TPU v7x, 32 devices: a whole 2x2x4 slice. The times are simulated.
32 devices in a mesh: seq: 8 (over z, x), tp: 4 (over y, core).
Axes of the slice: x: 2, y: 2, z: 4, core: 2. Of those that a mesh axis runs over, the one named last changes fastest.
Arguments:
- tokens: bfloat16 [16384, 2560], P('seq'), may hold values from -6 to 6
- w_query: bfloat16 [2560, 512], P(None, 'tp'), may hold values from -0.009765625 to 0.009765625
- w_key: bfloat16 [2560, 512], P(None, 'tp'), may hold values from -0.0009765625 to 0.0009765625
- w_value: bfloat16 [2560, 1024], P(None, 'tp'), may hold values from -0.125 to 0.125
- w_gate: bfloat16 [2560, 512], P(None, 'tp'), may hold values from -0.125 to 0.125
- gate_rate: float32 [512], P('tp'), may hold values from 1.5258789e-05 to 0.00012207031
- out_grad: bfloat16 [16384, 1024], P('seq', 'tp'), may hold values from -6 to 6
Outputs:
- input_grad: bfloat16 [16384, 2560], P(('seq', 'tp'))
- gate_signal: float32 [16384, 512], P('seq', 'tp')
All inputs are finite; a program needn't handle non-finite values.
Results may differ from a plain program's by a relative error of at most 0.015.
Values sent between devices are 32-bit elements.
A program may use at most 192 MiB of HBM per device.

v0:
```python
import math

import jax
import jax.numpy as jnp
from jax import lax
from jax.sharding import PartitionSpec as P

DK = 128
DV = 256
CH = 128


def prefix(value, axis, join, neutral, backward):
    count, mine = lax.axis_size(axis), lax.axis_index(axis)
    pieces = jax.tree.map(lambda part: lax.all_gather(part, axis), value)
    if backward:
        pieces = jax.tree.map(lambda part: part[::-1], pieces)
        mine = count - 1 - mine
    so_far = jax.tree.map(
        lambda part, zero: jnp.full_like(part, 0) + jnp.asarray(zero, part.dtype), value, neutral
    )

    def step(position, so_far):
        longer = join(so_far, jax.tree.map(lambda part: part[position], pieces))
        return jax.tree.map(lambda new, old: jnp.where(position < mine, new, old), longer, so_far)

    return lax.fori_loop(0, count - 1, step, so_far)


def lower_ones(length):
    places = jnp.arange(length)
    return (places[:, None] >= places[None, :]).astype(jnp.float32)


def low_dot(left, right):
    return jnp.dot(
        left.astype(jnp.bfloat16), right.astype(jnp.bfloat16), preferred_element_type=jnp.float32
    )


def run_head(query_rows, key_rows, value_rows, log_gate, initial):
    block_size = CH
    blocks_count = query_rows.shape[0] // block_size
    triangle = lower_ones(block_size)
    pieces = tuple(
        (
            a.reshape(blocks_count, block_size, a.shape[1])
            for a in (query_rows, key_rows, value_rows, log_gate)
        )
    )

    def advance(memory, piece):
        query_block, key_block, value_block, gate_block = piece
        within = jnp.cumsum(gate_block, axis=0)
        closing = within[-1]
        query_scaled = query_block * jnp.exp(within)
        key_scaled = key_block * jnp.exp(-within)
        scores = low_dot(query_scaled, key_scaled.T) * triangle
        output = low_dot(query_scaled, memory) + low_dot(scores, value_block)
        key_closing = key_block * jnp.exp(closing - within)
        memory = jnp.exp(closing)[:, None] * memory + low_dot(key_closing.T, value_block)
        return (memory, output)

    last_memory, outputs = lax.scan(advance, initial, pieces)
    return (outputs.reshape(-1, outputs.shape[2]), last_memory)


def by_heads(matrix, width):
    return matrix.astype(jnp.float32).reshape(matrix.shape[0], -1, width).transpose(1, 0, 2)


def by_tokens(stacked):
    return stacked.transpose(1, 0, 2).reshape(stacked.shape[1], -1)


def back_project(grad_rows, weight):
    return lax.dot_general(
        grad_rows, weight, (((1,), (1,)), ((), ())), preferred_element_type=jnp.float32
    )


def compose(earlier, later):
    return (later[0] * earlier[0], later[0][..., None] * earlier[1] + later[1])


def body(tokens, w_query, w_key, w_value, w_gate, gate_rate, out_grad):
    queries = jnp.dot(tokens, w_query, preferred_element_type=jnp.float32).astype(jnp.bfloat16)
    keys_proj = jnp.dot(tokens, w_key, preferred_element_type=jnp.float32).astype(jnp.bfloat16)
    values_proj = jnp.dot(tokens, w_value, preferred_element_type=jnp.float32).astype(jnp.bfloat16)
    squashed = jax.nn.sigmoid(jnp.dot(tokens, w_gate, preferred_element_type=jnp.float32))
    log_gate = -gate_rate * squashed
    query_heads = by_heads(queries, DK)
    key_heads = by_heads(keys_proj, DK)
    value_heads = by_heads(values_proj, DV)
    gate_heads = by_heads(log_gate, DK)
    grad_heads = by_heads(out_grad, DV)
    running = jnp.cumsum(log_gate, axis=0)
    total = running[-1]
    decay = jnp.exp(total).reshape(-1, DK)
    fed_keys = (keys_proj.astype(jnp.float32) * jnp.exp(total - running)).astype(jnp.bfloat16)
    fed_keys = fed_keys.reshape(fed_keys.shape[0], -1, DK)
    local_state = jnp.einsum(
        "lhd,lhe->hde",
        fed_keys,
        values_proj.reshape(values_proj.shape[0], -1, DV),
        preferred_element_type=jnp.float32,
    )
    fed_queries = (queries.astype(jnp.float32) * jnp.exp(running)).astype(jnp.bfloat16)
    fed_queries = fed_queries.reshape(fed_queries.shape[0], -1, DK)
    local_cotangent = jnp.einsum(
        "lhd,lhe->hde",
        fed_queries,
        out_grad.reshape(out_grad.shape[0], -1, DV),
        preferred_element_type=jnp.float32,
    )
    zero_state = jnp.zeros_like(local_state)
    identity = (jnp.ones_like(decay), zero_state)
    start_state = prefix((decay, local_state), "seq", compose, identity, False)[1]
    end_grad = prefix((decay, local_cotangent), "seq", compose, identity, True)[1]

    def local_run(query_part, key_part, value_part, gate_part):
        return jax.vmap(run_head)(query_part, key_part, value_part, gate_part, start_state)

    unused_outputs, pullback = jax.vjp(local_run, query_heads, key_heads, value_heads, gate_heads)
    grads = pullback((grad_heads, end_grad))
    query_grad = by_tokens(grads[0]).astype(jnp.bfloat16)
    key_grad = by_tokens(grads[1]).astype(jnp.bfloat16)
    value_grad = by_tokens(grads[2]).astype(jnp.bfloat16)
    pre_grad = by_tokens(grads[3]) * -gate_rate * squashed * (1.0 - squashed)
    whole_tokens = tokens.shape[0] * lax.axis_size("seq")
    gate_signal = pre_grad * (4.0 * math.sqrt(whole_tokens * DK / DV))
    gate_grad = pre_grad.astype(jnp.bfloat16)

    def term(rows_count):

        def rows_of(matrix):
            return lax.slice_in_dim(matrix, 0, rows_count, axis=0)

        mixed = back_project(rows_of(query_grad), w_query) + back_project(rows_of(key_grad), w_key)
        return (
            mixed
            + back_project(rows_of(value_grad), w_value)
            + back_project(rows_of(gate_grad), w_gate)
        )

    summed = lax.psum_scatter(
        term(tokens.shape[0] // lax.axis_size("tp") * lax.axis_size("tp")),
        "tp",
        scatter_dimension=0,
        tiled=True,
    )
    return (summed.astype(jnp.bfloat16), gate_signal)


def solution(mesh):
    placed = (
        P("seq", None),
        P(None, "tp"),
        P(None, "tp"),
        P(None, "tp"),
        P(None, "tp"),
        P("tp"),
        P("seq", "tp"),
    )
    return jax.shard_map(
        body,
        mesh=mesh,
        in_specs=placed,
        out_specs=(P(("seq", "tp"), None), P("seq", "tp")),
        check_vma=False,
    )
```

profile of v0, /device:TPU:0, one launch (start us, length us, event | category | flops | bytes accessed | tf_op | source)
XLA Modules:
  0.0 687.2 jit_solution(6645646297306001391)
XLA Ops:
  8.1 8.4 %fusion.91 = f32[2048,128]{1,0:T(8,128)} fusion(bf16[2048,2560]{1,0:T(8,128)(2,1)} %param.15, bf16[2560,128]{1,0:T(8,128)(2,1)} %param.16), kind=kOutput, calls=%fused_computation.143 | convolution fusion | flops 1342701568 | bytes 12189696 | tf_op jit(solution)/shard_map/dot_general | solution.py:87
  16.5 3.9 broadcast_multiply_fusion
  22.4 2.3 fusion.96
  24.8 5.8 fusion.90
  30.6 7.2 %convolution_convert_fusion.8 = bf16[2048,256]{1,0:T(8,128)(2,1)S(1)} fusion(bf16[2048,2560]{1,0:T(8,128)(2,1)} %param.15, bf16[2560,256]{1,0:T(8,128)(2,1)S(1)} %copy-done), kind=kOutput, calls=%fused_computation.135 | convolution fusion | flops 2684878848 | bytes 12845056 | tf_op jit(solution)/shard_map/dot_general | solution.py:89
  42.0 22.6 %all-gather.3 = f32[8,1,128]{2,1,0:T(1,128)S(1)} all-gather(f32[1,1,128]{2,1,0:T(1,128)S(1)} %get-tuple-element.1189), channel_id=2, replica_groups=mesh['seq'=8,'tp'=4] {'seq'}, dimensions={0}, use_global_device_ids=true | all-gather | bytes 4608 | tf_op jit(solution)/shard_map/all_gather | solution.py:15
  64.6 3.7 all-gather.7.cloned.1.call-done
  68.3 2.3 rev.7
  70.6 7.3 %while.96 = (s32[]{:T(128)}, f32[1,128,256]{2,1,0:T(8,128)S(1)}, s32[]{:T(128)}, f32[8,1,128]{2,1,0:T(1,128)S(1)}, f32[8,1,128,256]{3,2,1,0:T(8,128)}) while((s32[]{:T(128)}, f32[1,128,256]{2,1,0:T(8,128)S(1)}, s32[]{:T(128)}, f32[8,1,128]{2,1,0:T(1,128)S(1)}, f32[8,1,128,256]{3,2,1,0:T(8,128)}) %tuple.204), condition=%wide.region_3.4_spmd.clone.clone, body=%wide.region_2.3_spmd.clone.sunk.clone | while | flops 131076 | bytes 394849 | solution.py:27
  78.0 31.7 %all-gather.9.cloned.1.call-done = f32[1024,256]{1,0:T(8,128)} async-done(((f32[128,256]{1,0:T(8,128)}), f32[1024,256]{1,0:T(8,128)}) %all-gather.9.cloned.1.call-update) | async-done | bytes 1048592 | tf_op jit(solution)/shard_map/all_gather | solution.py:15
  109.6 7.3 %while.97 = (s32[]{:T(128)}, f32[1,128,256]{2,1,0:T(8,128)S(1)}, s32[]{:T(128)}, f32[8,1,128]{2,1,0:T(1,128)S(1)}, f32[8,1,128,256]{3,2,1,0:T(8,128)}) while((s32[]{:T(128)}, f32[1,128,256]{2,1,0:T(8,128)S(1)}, s32[]{:T(128)}, f32[8,1,128]{2,1,0:T(1,128)S(1)}, f32[8,1,128,256]{3,2,1,0:T(8,128)}) %tuple.203), condition=%wide.region_5.6_spmd.clone.clone, body=%wide.region_4.5_spmd.clone.sunk.clone | while | flops 131076 | bytes 394849 | solution.py:27
  120.3 138.9 %while.94 = (s32[]{:T(128)}, f32[1,128,256]{2,1,0:T(8,128)S(1)}, f32[16,1,128,128]{3,2,1,0:T(8,128)}, f32[16,1,128,128]{3,2,1,0:T(8,128)}, bf16[16,1,128,128]{2,...) while((s32[]{:T(128)}, f32[1,128,256]{2,1,0:T(8,128)S(1)}, ...), condition=%wide.region_8.9_spmd.clone.clone, body=%wide.region_6.8_spmd.clone.sunk.clone | while | flops 14991362 | bytes 2036953 | solution.py:64
  260.4 210.2 %while.95 = (s32[]{:T(128)}, f32[1,128,256]{1,2,0:T(8,128)S(1)}, bf16[16,1,128,128]{3,2,1,0:T(8,128)(2,1)S(1)}, bf16[16,1,128,128]{3,2,1,0:T(8,128)(2,1)}, bf16[...) while((s32[]{:T(128)}, f32[1,128,256]{1,2,0:T(8,128)S(1)}, ...), condition=%wide.region_13.14_spmd.clone.clone, body=%wide.region_9.13_spmd.clone.sunk.clone | while | flops 61521920 | bytes 4141797 | solution.py:64
  267.5 1.7 bitcast_dynamic-update-slice_fusion.20
  320.0 1.7 bitcast_dynamic-update-slice_fusion.20
  333.2 1.7 bitcast_dynamic-update-slice_fusion.20
  346.3 1.7 bitcast_dynamic-update-slice_fusion.20
  359.4 1.7 bitcast_dynamic-update-slice_fusion.20
  372.6 1.7 bitcast_dynamic-update-slice_fusion.20
  385.7 1.7 bitcast_dynamic-update-slice_fusion.20
  398.9 1.7 bitcast_dynamic-update-slice_fusion.20
  412.0 1.7 bitcast_dynamic-update-slice_fusion.20
  425.2 1.7 bitcast_dynamic-update-slice_fusion.20
  438.3 1.7 bitcast_dynamic-update-slice_fusion.20
  451.4 1.7 bitcast_dynamic-update-slice_fusion.20
  464.6 1.7 bitcast_dynamic-update-slice_fusion.20
  470.6 10.0 %fusion.112 = f32[2048,2560]{1,0:T(8,128)} fusion(bf16[2048,256]{1,0:T(8,128)(2,1)} %bitcast.510, bf16[2560,256]{1,0:T(8,128)(2,1)S(1)} %copy-done), kind=kOutput, calls=%fused_computation.167 | convolution fusion | flops 2684354560 | bytes 23330816 | tf_op jit(solution)/shard_map/dot_general | solution.py:77
  480.6 8.6 %fusion.110 = f32[2048,2560]{1,0:T(8,128)} fusion(bf16[2048,128]{1,0:T(8,128)(2,1)S(1)} %bitcast.509, bf16[2560,128]{1,0:T(8,128)(2,1)S(1)} %copy-done.9), kind=kOutput, calls=%fused_computation.165 | convolution fusion | flops 1342177280 | bytes 22151168 | tf_op jit(solution)/shard_map/dot_general | solution.py:77
  489.3 8.6 %fusion.111 = f32[2048,2560]{1,0:T(8,128)} fusion(bf16[2048,128]{1,0:T(8,128)(2,1)S(1)} %bitcast.514, bf16[2560,128]{1,0:T(8,128)(2,1)S(1)} %copy-done.10), kind=kOutput, calls=%fused_computation.166 | convolution fusion | flops 1342177280 | bytes 22151168 | tf_op jit(solution)/shard_map/dot_general | solution.py:77
  499.1 28.1 %add_add_fusion = f32[2048,2560]{1,0:T(8,128)} fusion(f32[2048,2560]{1,0:T(8,128)} %fusion.112, f32[2048,2560]{1,0:T(8,128)} %fusion.110, f32[2048,2560]{1,0:T(8,128)} %fusion.111, bf16[2560,128]{1,0:T(8,128)(2,1)S(1)} %copy-done.12, bf16[2048,128]{1,0:T(8,128)(2,1)S(1)} %get-tuple-element.1172), kind=kOutput, calls=%fused_computation.134 | convolution fusion | flops 1357905920 | bytes 85065728 | tf_op jit(solution)/shard_map/dot_general | solution.py:77
  527.3 149.1 %reduce-scatter.2.cloned.1.call-done = f32[512,2560]{1,0:T(8,128)} async-done(((f32[2048,2560]{1,0:T(8,128)}), f32[512,2560]{1,0:T(8,128)}) %reduce-scatter.2.cloned.1.call-update) | async-done | bytes 5242896 | tf_op jit(solution)/shard_map/reduce_scatter | solution.py:146
  676.4 4.3 convert_element_type.319
  (527 shorter events, 353.2 us)
Async XLA Ops:
  7.2 23.4 %copy-start = (bf16[2560,256]{1,0:T(8,128)(2,1)S(1)}, bf16[2560,256]{1,0:T(8,128)(2,1)}, u32[]{:S(2)}) copy-start(bf16[2560,256]{1,0:T(8,128)(2,1)} %param.18) | copy-start | bytes 3932164
  7.2 9.3 %copy-start.11 = (bf16[2560,128]{1,0:T(8,128)(2,1)S(1)}, bf16[2560,128]{1,0:T(8,128)(2,1)}, u32[]{:S(2)}) copy-start(bf16[2560,128]{1,0:T(8,128)(2,1)} %param.19) | copy-start | bytes 1966084
  7.2 61.1 %all-gather.7.cloned.1.call-start = ((), (), s32[]{:S(2)}) async-start(), calls=%async_computation.2 | async-start | bytes 1179648 | tf_op jit(solution)/shard_map/all_gather | solution.py:15
  7.2 9.3 %copy-start.13 = (bf16[2048,2560]{1,0:T(8,128)(2,1)S(1)}, bf16[2048,2560]{1,0:T(8,128)(2,1)}, u32[]{:S(2)}) copy-start(bf16[2048,2560]{1,0:T(8,128)(2,1)} %param.15) | copy-start | bytes 31457284
  16.5 5.9 copy-start.2
  20.4 1.0 copy-start.7
  24.7 84.9 %all-gather.9.cloned.1.call-start = ((), (), s32[]{:S(2)}) async-start(), calls=%async_computation.3 | async-start | bytes 1179648 | tf_op jit(solution)/shard_map/all_gather | solution.py:15
  30.6 7.3 %copy-start.4 = (f32[2048,128]{1,0:T(8,128)}, f32[2048,128]{1,0:T(8,128)S(1)}, u32[]{:S(2)}) copy-start(f32[2048,128]{1,0:T(8,128)S(1)} %fusion.90) | copy-start | bytes 3145732
  37.8 1.0 copy-start.5
  39.9 636.5 %reduce-scatter.2.cloned.1.call-start = ((), (), s32[]{:S(2)}) async-start(), calls=%async_computation.1 | async-start | bytes 26214400 | tf_op jit(solution)/shard_map/reduce_scatter | solution.py:146
  470.6 10.0 %copy-start.9 = (bf16[2560,128]{1,0:T(8,128)(2,1)S(1)}, bf16[2560,128]{1,0:T(8,128)(2,1)}, u32[]{:S(2)}) copy-start(bf16[2560,128]{1,0:T(8,128)(2,1)} %param.16) | copy-start | bytes 1966084
  480.6 8.7 %copy-start.6 = (bf16[16,1,128,128]{3,2,1,0:T(8,128)(2,1)S(1)}, bf16[16,1,128,128]{3,2,1,0:T(8,128)(2,1)}, u32[]{:S(2)}) copy-start(bf16[16,1,128,128]{3,2,1,0:T(8,128)(2,1)} %get-tuple-element.848) | copy-start | bytes 1572868
  480.6 8.7 %copy-start.10 = (bf16[2560,128]{1,0:T(8,128)(2,1)S(1)}, bf16[2560,128]{1,0:T(8,128)(2,1)}, u32[]{:S(2)}) copy-start(bf16[2560,128]{1,0:T(8,128)(2,1)} %param.17) | copy-start | bytes 1966084
  489.3 8.7 %copy-start.3 = (f32[16,1,128,128]{3,2,1,0:T(8,128)S(1)}, f32[16,1,128,128]{3,2,1,0:T(8,128)}, u32[]{:S(2)}) copy-start(f32[16,1,128,128]{3,2,1,0:T(8,128)} %get-tuple-element.850) | copy-start | bytes 3145732
  489.3 8.7 %copy-start.8 = (f32[2048,128]{1,0:T(8,128)S(1)}, f32[2048,128]{1,0:T(8,128)}, u32[]{:S(2)}) copy-start(f32[2048,128]{1,0:T(8,128)} %get-tuple-element.1193) | copy-start | bytes 3145732
  489.3 9.8 %copy-start.12 = (bf16[2560,128]{1,0:T(8,128)(2,1)S(1)}, bf16[2560,128]{1,0:T(8,128)(2,1)}, u32[]{:S(2)}) copy-start(bf16[2560,128]{1,0:T(8,128)(2,1)} %param.19) | copy-start | bytes 1966084
  527.3 153.4 %copy-start.1 = (bf16[2560,256]{1,0:T(8,128)(2,1)S(1)}, bf16[2560,256]{1,0:T(8,128)(2,1)}, u32[]{:S(2)}) copy-start(bf16[2560,256]{1,0:T(8,128)(2,1)} %param.18) | copy-start | bytes 3932164
Sparse Core Ops, SparseCore 0:
  24.8 43.3 all-gather.6
  70.4 39.2 all-gather.8
  527.4 148.9 reduce-scatter.1
where the time goes:
time: 700 us; the launch traced here: 687 us
  matrix products  261 us (37%)
  waiting for transfers between devices  184 us (26%)
  other arithmetic  142 us (20%)
  local copies, waits for them, and re-layouts  61 us (9%)
  blocking collectives  22.6 us (3%)
  between operations  14 us (2%)
    dot_general x160, matrix products, low_dot(): jnp.dot(left.astype(jnp.bfloat16), right.astype(jnp.bfloat16), preferred_...  177 us
    reduce_scatter x1, waiting for transfers between devices, body(): lax.psum_scatter(term(tokens.shape[0] // lax.axis_size('tp') * lax.axis_s...  149 us
    dynamic_update_slice x64, other arithmetic, run_head(): last_memory, outputs = lax.scan(advance, initial, pieces)  82.4 us
    dot_general x4, matrix products, back_project(): lax.dot_general(grad_rows, weight, (((1,), (1,)), ((), ())), preferred_el...  55.4 us
    another operation x48, other arithmetic, advance(): within = jnp.cumsum(gate_block, axis=0)  36.6 us
    all_gather x2, waiting for transfers between devices, prefix(): pieces = jax.tree.map(lambda part: lax.all_gather(part, axis), value)  35.3 us
    all_gather x1, blocking collectives, prefix(): pieces = jax.tree.map(lambda part: lax.all_gather(part, axis), value)  22.6 us
    dynamic_update_slice x64, local copies, waits for them, and re-layouts, run_head(): last_memory, outputs = lax.scan(advance, initial, pieces)  21 us
  transfers between devices with their start and end apart: 3, of which 3 were waited for; matrix products, arithmetic and copies ran while one was open for 4% of the time, Pallas kernels for 0%

commit v1 on v0

v1 whole, which is shorter than its diff:
```python
import functools
import math

import jax
import jax.numpy as jnp
from jax import lax
from jax.experimental import pallas as pl
from jax.experimental.pallas import tpu as pltpu
from jax.sharding import PartitionSpec as P

CH = 128
PAD = 8
VMEM_LIMIT = 66 * 1000 * 1000
F32, BF16 = jnp.float32, jnp.bfloat16


def mm(left, right, dims):
    return lax.dot_general(left, right, (dims, ((), ())), preferred_element_type=F32)


NN = ((1,), (0,))
NT = ((1,), (1,))
TN = ((0,), (0,))


def tri_sum(triangle, rows):
    high = rows.astype(BF16)
    low = (rows - high.astype(F32)).astype(BF16)
    return mm(triangle, high, NN) + mm(triangle, low, NN)


def kernel(
    seq, tp, dk, dv, tile, scale,
    tok, wq, wk, wv, wg, rate_ref, dout_ref,
    grad_ref, sig_ref,
    wcat, xbuf, proj, sq_all, w_all, s_all, m_all, cl_all, msg, got, edge,
    send_a, recv_a, send_y, recv_y, send_b, recv_b,
    w_sem, x_sem, msg_send, msg_recv, sa_sem, ra_sem, sy_sem, ry_sem, sb_sem, rb_sem,
):
    me, rank = lax.axis_index("seq"), lax.axis_index("tp")
    length, width = dout_ref.shape[0], wcat.shape[0]
    blocks, tiles = length // CH, length // tile
    each = blocks // tp
    core = rank + 1 - 2 * lax.rem(rank, 2)
    far = lax.rem(rank + 2, 4)
    far_core = lax.rem(core + 2, 4)

    def x_copy(t, slot):
        return pltpu.make_async_copy(
            tok.at[pl.ds(pl.multiple_of(t * tile, tile), tile), :], xbuf.at[slot], x_sem.at[slot]
        )

    loads = []
    for n, (w, start, size) in enumerate(
        ((wq, 0, dk), (wk, dk, dk), (wv, 2 * dk, dv), (wg, 2 * dk + dv, dk))
    ):
        loads.append(pltpu.make_async_copy(w, wcat.at[:, pl.ds(start, size)], w_sem.at[n]))
    x_copy(0, 0).start()
    for load in loads:
        load.start()

    barrier = pltpu.get_barrier_semaphore()
    for d in range(1, seq):
        pl.semaphore_signal(
            barrier, inc=1, device_id={"seq": lax.rem(me + d, seq)},
            device_id_type=pl.DeviceIdType.MESH,
        )
    for other in (core, far):
        pl.semaphore_signal(
            barrier, inc=1, device_id={"tp": other}, device_id_type=pl.DeviceIdType.MESH
        )

    rows_at = lax.broadcasted_iota(jnp.int32, (CH, CH), 0)
    cols_at = lax.broadcasted_iota(jnp.int32, (CH, CH), 1)
    lower = (rows_at >= cols_at).astype(F32)
    lower_b = lower.astype(BF16)
    upper_b = (rows_at <= cols_at).astype(BF16)
    rate = rate_ref[...]

    zero_state = jnp.zeros((dv, dk), F32)
    msg[0, pl.ds(0, dv), :] = zero_state
    msg[1, pl.ds(0, dv), :] = zero_state
    for load in loads:
        load.wait()

    def project(t, total):
        slot = lax.rem(t, 2)

        @pl.when(t + 1 < tiles)
        def _():
            x_copy(t + 1, 1 - slot).start()

        x_copy(t, slot).wait()
        out = mm(xbuf[slot], wcat[...], NN)
        base = pl.multiple_of(t * tile, tile)
        proj[pl.ds(base, tile), :] = out[:, : 2 * dk + dv].astype(BF16)
        squashed = jax.nn.sigmoid(out[:, 2 * dk + dv :])
        sq_all[pl.ds(base, tile), :] = squashed
        for j in range(tile // CH):
            part = slice(j * CH, (j + 1) * CH)
            b = t * (tile // CH) + j
            within = tri_sum(lower_b, -rate * squashed[part])
            w_all[pl.ds(pl.multiple_of(base + j * CH, CH), CH), :] = within
            closing = within[CH - 1 : CH]
            cl_all[b] = jnp.broadcast_to(closing, (PAD, dk))
            query = out[part, :dk].astype(BF16).astype(F32)
            key = out[part, dk : 2 * dk].astype(BF16).astype(F32)
            value = out[part, 2 * dk : 2 * dk + dv].astype(BF16)
            dout = dout_ref[pl.ds(pl.multiple_of(base + j * CH, CH), CH), :]
            query_scaled = (query * jnp.exp(within)).astype(BF16)
            key_closing = (key * jnp.exp(closing - within)).astype(BF16)
            state = msg[0, pl.ds(0, dv), :]
            s_all[b] = state
            msg[0, pl.ds(0, dv), :] = jnp.exp(closing) * state + mm(value, key_closing, TN)
            fed = mm(dout, query_scaled, TN)
            m_all[b] = fed
            msg[1, pl.ds(0, dv), :] += jnp.exp(total) * fed
            total = total + closing
        return total

    total = lax.fori_loop(0, tiles, project, jnp.zeros((1, dk), F32))
    decay = jnp.broadcast_to(jnp.exp(total), (PAD, dk))
    msg[0, pl.ds(dv, PAD), :] = decay
    msg[1, pl.ds(dv, PAD), :] = decay

    pl.semaphore_wait(barrier, seq + 1)

    def exchange(d):
        return pltpu.make_async_remote_copy(
            src_ref=msg.at[(me + d) // seq],
            dst_ref=got.at[d],
            send_sem=msg_send.at[d],
            recv_sem=msg_recv.at[d],
            device_id={"seq": lax.rem(me + d, seq)},
            device_id_type=pl.DeviceIdType.MESH,
        )

    def start_exchange(d, carry):
        exchange(d).start()
        return carry

    def wait_exchange(d, carry):
        exchange(d).wait()
        return carry

    lax.fori_loop(1, seq, start_exchange, 0)
    lax.fori_loop(1, seq, wait_exchange, 0)

    edge[...] = jnp.zeros_like(edge)

    def fold(which, d):
        edge[which] = got[d, pl.ds(dv, 1), :] * edge[which] + got[d, pl.ds(0, dv), :]

    def fold_states(j, carry):
        fold(0, me - j)
        return carry

    def fold_grads(d, carry):
        fold(1, d)
        return carry

    lax.fori_loop(0, me, fold_states, 0)
    lax.fori_loop(me + 1, seq, fold_grads, 0)

    def enter(b, so_far):
        s_all[b] = s_all[b] + jnp.exp(so_far) * edge[0]
        return so_far + cl_all[b, 0:1, :]

    lax.fori_loop(0, blocks, enter, jnp.zeros((1, dk), F32))

    def leave(j, carry):
        b = blocks - 1 - j
        fed = m_all[b]
        leaving = edge[1]
        m_all[b] = leaving
        edge[1] = jnp.exp(cl_all[b, 0:1, :]) * leaving + fed
        return carry

    lax.fori_loop(0, blocks, leave, 0)

    def grads(b):
        rows = pl.ds(pl.multiple_of(b * CH, CH), CH)
        query = proj[rows, 0:dk].astype(F32)
        key = proj[rows, dk : 2 * dk].astype(F32)
        value = proj[rows, 2 * dk : 2 * dk + dv]
        within, squashed, dout = w_all[rows, :], sq_all[rows, :], dout_ref[rows, :]
        closing = within[CH - 1 : CH]
        state, leaving = s_all[b], m_all[b]
        grow, shrink, rest = jnp.exp(within), jnp.exp(-within), jnp.exp(closing - within)
        query_f, key_f, close_f = query * grow, key * shrink, key * rest
        query_s, key_s, close_s = query_f.astype(BF16), key_f.astype(BF16), close_f.astype(BF16)
        scores = (mm(query_s, key_s, NT) * lower).astype(BF16)
        d_scores = (mm(dout, value, NT) * lower).astype(BF16)
        leaving_b = leaving.astype(BF16)
        d_query_s = mm(dout, state.astype(BF16), NN) + mm(d_scores, key_s, NN)
        d_key_s = mm(d_scores, query_s, TN)
        d_close = mm(value, leaving_b, NN)
        d_value = mm(scores, dout, TN) + mm(close_s, leaving_b, NT)
        d_query = d_query_s * grow
        d_key = d_key_s * shrink + d_close * rest
        at_close = d_close * close_f
        d_within = d_query_s * query_f - d_key_s * key_f - at_close
        d_closing = jnp.sum(at_close, axis=0, keepdims=True) + jnp.exp(closing) * jnp.sum(
            leaving * state, axis=0, keepdims=True
        )
        d_gate = tri_sum(upper_b, d_within) + d_closing
        pre = d_gate * -rate * squashed * (1.0 - squashed)
        sig_ref[rows, :] = pre * scale
        return jnp.concatenate(
            [d_query.astype(BF16), d_key.astype(BF16), d_value.astype(BF16), pre.astype(BF16)],
            axis=1,
        )

    step = 512 if width % 512 == 0 else width

    def spread(packed, put):
        for at in range(0, width, step):
            cols = slice(at, at + step)
            put(cols, mm(packed, wcat[cols, :], NT))

    def remote(src, dst, sent, came, i, other):
        return pltpu.make_async_remote_copy(
            src_ref=src.at[i], dst_ref=dst.at[i], send_sem=sent.at[i], recv_sem=came.at[i],
            device_id={"tp": other}, device_id_type=pl.DeviceIdType.MESH,
        )

    def copy_a(i):
        return remote(send_a, recv_a, sa_sem, ra_sem, i, core)

    def copy_y(i):
        return remote(send_y, recv_y, sy_sem, ry_sem, i, far)

    def copy_b(i):
        return remote(send_b, recv_b, sb_sem, rb_sem, i, core)

    def away(i, carry):
        packed = grads(far_core * each + i)

        def put_a(cols, part):
            send_a[i, :, cols] = part

        spread(packed, put_a)
        copy_a(i).start()
        packed = grads(far * each + i)
        copy_a(i).wait()

        def put_y(cols, part):
            send_y[i, :, cols] = part + recv_a[i, :, cols]

        spread(packed, put_y)
        copy_y(i).start()
        return carry

    lax.fori_loop(0, each, away, 0)

    def home(i, carry):
        packed = grads(core * each + i)

        def put_b(cols, part):
            send_b[i, :, cols] = part

        spread(packed, put_b)
        copy_b(i).start()
        packed = grads(rank * each + i)
        copy_b(i).wait()

        def put_own(cols, part):
            send_a[i, :, cols] = part + recv_b[i, :, cols]

        spread(packed, put_own)
        return carry

    lax.fori_loop(0, each, home, 0)

    def finish(i, carry):
        copy_y(i).wait()
        rows = pl.ds(pl.multiple_of(i * CH, CH), CH)
        grad_ref[rows, :] = (send_a[i] + recv_y[i]).astype(BF16)
        return carry

    lax.fori_loop(0, each, finish, 0)


def solution(mesh):
    seq, tp = mesh.shape["seq"], mesh.shape["tp"]

    def body(tokens, w_query, w_key, w_value, w_gate, gate_rate, out_grad):
        length, width = tokens.shape
        dk, dv = w_query.shape[1], w_value.shape[1]
        blocks, each = length // CH, length // CH // tp
        tile = 2 * CH
        scale = 4.0 * math.sqrt(length * seq * dk / dv)
        piece = (each, CH, width)
        hbm = pl.BlockSpec(memory_space=pl.ANY)
        vmem = pl.BlockSpec(memory_space=pltpu.VMEM)
        dma = pltpu.SemaphoreType.DMA
        return pl.pallas_call(
            functools.partial(kernel, seq, tp, dk, dv, tile, scale),
            out_shape=(
                jax.ShapeDtypeStruct((length // tp, width), BF16),
                jax.ShapeDtypeStruct((length, dk), F32),
            ),
            in_specs=[hbm] * 5 + [vmem] * 2,
            out_specs=(vmem, vmem),
            scratch_shapes=[
                pltpu.VMEM((width, 3 * dk + dv), BF16),
                pltpu.VMEM((2, tile, width), BF16),
                pltpu.VMEM((length, 2 * dk + dv), BF16),
                pltpu.VMEM((length, dk), F32),
                pltpu.VMEM((length, dk), F32),
                pltpu.VMEM((blocks, dv, dk), F32),
                pltpu.VMEM((blocks, dv, dk), F32),
                pltpu.VMEM((blocks, PAD, dk), F32),
                pltpu.VMEM((2, dv + PAD, dk), F32),
                pltpu.VMEM((seq, dv + PAD, dk), F32),
                pltpu.VMEM((2, dv, dk), F32),
            ]
            + [pltpu.VMEM(piece, F32)] * 6
            + [dma((4,)), dma((2,)), dma((seq,)), dma((seq,))]
            + [dma((each,))] * 6,
            compiler_params=pltpu.CompilerParams(
                collective_id=0, has_side_effects=True, vmem_limit_bytes=VMEM_LIMIT
            ),
        )(tokens, w_query, w_key, w_value, w_gate, gate_rate.reshape(1, dk), out_grad)

    placed = (
        P("seq", None),
        P(None, "tp"),
        P(None, "tp"),
        P(None, "tp"),
        P(None, "tp"),
        P("tp"),
        P("seq", "tp"),
    )
    return jax.shard_map(
        body,
        mesh=mesh,
        in_specs=placed,
        out_specs=(P(("seq", "tp"), None), P("seq", "tp")),
        check_vma=False,
    )
```

time: 700 us -> 172 us (0.25)
  the two profiles are of different devices: /device:TPU:0 before, /device:TPU:9 now
where the time goes in v1:
time: 172 us; the launch traced here: 170 us
  Pallas kernels  165 us (96%)
  local copies, waits for them, and re-layouts  4.46 us (3%)
    pallas_call x1, Pallas kernels, body(): pl.pallas_call(functools.partial(kernel, seq, tp, dk, dv, tile, scale), o...  165 us
    unnamed x4, local copies, waits for them, and re-layouts  4.46 us

profile of v1, /device:TPU:9, one launch (start us, length us, event | category | flops | bytes accessed | tf_op | source)
XLA Modules:
  0.0 170.1 jit_solution(11971941696090390291)
XLA Ops:
  0.6 165.0 %shard_map.86 = (bf16[512,2560]{1,0:T(8,128)(2,1)}, f32[2048,128]{1,0:T(8,128)}) custom-call(bf16[2048,2560]{1,0:T(8,128)(2,1)} %tok.1, bf16[2560,128]{1,0:T(8,128)(2,1)} %wq.1, bf16[2560,128]{1,0:T(8,128)(2,1)} %wk.1, bf16[2560,256]{1,0:T(8,128)(2,1)} %wv.1, bf16[2560,128]{1,0:T(8,128)(2,1)} %wg.1, f32[1,128]{1,0:T(1,128)} %bitcast.1, ...), custom_call_target="tpu_custom_call" | custom-call | tf_op jit(solution)/shard_map/pallas_call | solution.py:297
  165.7 0.0 copy-start
  165.7 3.5 %copy.11 = bf16[512,2560]{1,0:T(8,128)(2,1)} copy(bf16[512,2560]{1,0:T(8,128)(2,1)} %get-tuple-element.4) | data formatting | bytes 5242880
  169.2 0.0 copy-done
  169.2 1.0 copy.12
Async XLA Ops:
  165.7 3.5 %copy-start = (f32[2048,128]{1,0:T(8,128)S(1)}, f32[2048,128]{1,0:T(8,128)}, u32[]{:S(2)}) copy-start(f32[2048,128]{1,0:T(8,128)} %get-tuple-element.5) | copy-start | bytes 3145732

commit v2 on v1

--- a/solution.py
+++ b/solution.py
@@ -34,8 +34,8 @@
     tok, wq, wk, wv, wg, rate_ref, dout_ref,
     grad_ref, sig_ref,
     wcat, xbuf, proj, sq_all, w_all, s_all, m_all, cl_all, msg, got, edge,
-    send_a, recv_a, send_y, recv_y, send_b, recv_b,
-    w_sem, x_sem, msg_send, msg_recv, sa_sem, ra_sem, sy_sem, ry_sem, sb_sem, rb_sem,
+    wout0, wout1, land0, land1, wfar, g_own, g_send, g_recv, part_own, part_send, part_recv,
+    w_sem, x_sem, msg_send, msg_recv, gs_sem, gr_sem, ps_sem, pr_sem, first_sem, ring_s, ring_r,
 ):
     me, rank = lax.axis_index("seq"), lax.axis_index("tp")
     length, width = dout_ref.shape[0], wcat.shape[0]
@@ -44,6 +44,39 @@
     core = rank + 1 - 2 * lax.rem(rank, 2)
     far = lax.rem(rank + 2, 4)
     far_core = lax.rem(core + 2, 4)
+    half_ring, row = seq // 2, me // 2
+    place = row + lax.rem(me, 2) * (seq - 1 - 2 * row)
+    depth = width // seq
+
+    def seq_at(p):
+        p = lax.rem(p + seq, seq)
+        return 2 * p + (p // half_ring) * (2 * seq - 1 - 4 * p)
+
+    onward = (seq_at(place + 1), seq_at(place - 1))
+    wouts, lands = (wout0, wout1), (land0, land1)
+    starts = (0, wout0.shape[0])
+
+    def cross(way):
+        return pltpu.make_async_remote_copy(
+            src_ref=wouts[way], dst_ref=lands[way].at[0], send_sem=first_sem.at[way],
+            recv_sem=ring_r.at[way, 0], device_id={"tp": far},
+            device_id_type=pl.DeviceIdType.MESH,
+        )
+
+    def ring(way, k):
+        return pltpu.make_async_remote_copy(
+            src_ref=lands[way].at[k], dst_ref=lands[way].at[k + 1], send_sem=ring_s.at[way, k],
+            recv_sem=ring_r.at[way, k + 1], device_id={"seq": onward[way]},
+            device_id_type=pl.DeviceIdType.MESH,
+        )
+
+    def pump(k):
+        for way in (0, 1):
+            if isinstance(k, int) and k == 0:
+                cross(way).wait_recv()
+            else:
+                ring(way, k - 1).wait_recv()
+            ring(way, k).start()
 
     def x_copy(t, slot):
         return pltpu.make_async_copy(
@@ -82,6 +115,13 @@
     msg[1, pl.ds(0, dv), :] = zero_state
     for load in loads:
         load.wait()
+    for way in (0, 1):
+        size = wouts[way].shape[0]
+        at = pl.multiple_of(me * depth + starts[way], 16)
+        wouts[way][...] = wcat[pl.ds(at, size), :].astype(F32)
+    pl.semaphore_wait(barrier, seq + 1)
+    for way in (0, 1):
+        cross(way).start()
 
     def project(t, total):
         slot = lax.rem(t, 2)
@@ -123,8 +163,6 @@
     msg[0, pl.ds(dv, PAD), :] = decay
     msg[1, pl.ds(dv, PAD), :] = decay
 
-    pl.semaphore_wait(barrier, seq + 1)
-
     def exchange(d):
         return pltpu.make_async_remote_copy(
             src_ref=msg.at[(me + d) // seq],
@@ -144,7 +182,9 @@
         return carry
 
     lax.fori_loop(1, seq, start_exchange, 0)
+    pump(0)
     lax.fori_loop(1, seq, wait_exchange, 0)
+    pump(1)
 
     edge[...] = jnp.zeros_like(edge)
 
@@ -206,79 +246,135 @@
         d_gate = tri_sum(upper_b, d_within) + d_closing
         pre = d_gate * -rate * squashed * (1.0 - squashed)
         sig_ref[rows, :] = pre * scale
-        return jnp.concatenate(
-            [d_query.astype(BF16), d_key.astype(BF16), d_value.astype(BF16), pre.astype(BF16)],
-            axis=1,
-        )
-
+        return d_query, d_key, d_value, pre
+
+    bounds = ((0, dk), (dk, 2 * dk), (2 * dk, 2 * dk + dv), (2 * dk + dv, 3 * dk + dv))
     step = 512 if width % 512 == 0 else width
 
-    def spread(packed, put):
+    def spread(packed, weight, put):
         for at in range(0, width, step):
             cols = slice(at, at + step)
-            put(cols, mm(packed, wcat[cols, :], NT))
-
-    def remote(src, dst, sent, came, i, other):
+            put(cols, mm(packed, weight[cols, :], NT))
+
+    def copy_g(i):
         return pltpu.make_async_remote_copy(
-            src_ref=src.at[i], dst_ref=dst.at[i], send_sem=sent.at[i], recv_sem=came.at[i],
-            device_id={"tp": other}, device_id_type=pl.DeviceIdType.MESH,
-        )
-
-    def copy_a(i):
-        return remote(send_a, recv_a, sa_sem, ra_sem, i, core)
-
-    def copy_y(i):
-        return remote(send_y, recv_y, sy_sem, ry_sem, i, far)
-
-    def copy_b(i):
-        return remote(send_b, recv_b, sb_sem, rb_sem, i, core)
-
-    def away(i, carry):
-        packed = grads(far_core * each + i)
-
-        def put_a(cols, part):
-            send_a[i, :, cols] = part
-
-        spread(packed, put_a)
-        copy_a(i).start()
-        packed = grads(far * each + i)
-        copy_a(i).wait()
-
-        def put_y(cols, part):
-            send_y[i, :, cols] = part + recv_a[i, :, cols]
-
-        spread(packed, put_y)
-        copy_y(i).start()
-        return carry
-
-    lax.fori_loop(0, each, away, 0)
-
-    def home(i, carry):
-        packed = grads(core * each + i)
-
-        def put_b(cols, part):
-            send_b[i, :, cols] = part
-
-        spread(packed, put_b)
-        copy_b(i).start()
-        packed = grads(rank * each + i)
-        copy_b(i).wait()
+            src_ref=g_send.at[i], dst_ref=g_recv.at[i], send_sem=gs_sem.at[i],
+            recv_sem=gr_sem.at[i], device_id={"tp": far}, device_id_type=pl.DeviceIdType.MESH,
+        )
+
+    def copy_p(i):
+        return pltpu.make_async_remote_copy(
+            src_ref=part_send.at[i], dst_ref=part_recv.at[i], send_sem=ps_sem.at[i],
+            recv_sem=pr_sem.at[i], device_id={"tp": core}, device_id_type=pl.DeviceIdType.MESH,
+        )
+
+    def away(chunk, base):
+        def run(i, carry):
+            for (lo, hi), part in zip(bounds, grads(chunk * each + i)):
+                g_send[base + i, :, lo:hi] = part
+            copy_g(base + i).start()
+            return carry
+
+        lax.fori_loop(0, each, run, 0)
+
+    def home(chunk, base):
+        def run(i, carry):
+            for (lo, hi), part in zip(bounds, grads(chunk * each + i)):
+                g_own[base + i, :, lo:hi] = part.astype(BF16)
+            return carry
+
+        lax.fori_loop(0, each, run, 0)
+
+    steps = iter(range(2, seq - 1))
+
+    def pump_next():
+        k = next(steps, None)
+        if k is not None:
+            pump(k)
+
+    def rows_of(buffer, i):
+        return jnp.concatenate([buffer[2 * i], buffer[2 * i + 1]], axis=0).astype(BF16)
+
+    half = each // 2
+
+    away(far_core, 0)
+    pump_next()
+    away(far, each)
+    pump_next()
+    home(core, 0)
+    pump_next()
+    home(rank, each)
+    pump_next()
+
+    def own_part(i, carry):
+        def put_send(cols, part):
+            part_send[i, :, cols] = part
 
         def put_own(cols, part):
-            send_a[i, :, cols] = part + recv_b[i, :, cols]
-
-        spread(packed, put_own)
-        return carry
-
-    lax.fori_loop(0, each, home, 0)
+            part_own[i, :, cols] = part
+
+        spread(rows_of(g_own, i), wcat, put_send)
+        spread(rows_of(g_own, half + i), wcat, put_own)
+        return carry
+
+    lax.fori_loop(0, half, own_part, 0)
+    done = next(steps, seq - 1)
+
+    def pump_rest(k, carry):
+        pump(k)
+        return carry
+
+    lax.fori_loop(done, seq - 1, pump_rest, 0)
+    for way in (0, 1):
+        ring(way, seq - 2).wait_recv()
+
+    def unpack(k, carry):
+        for way in (0, 1):
+            origin = seq_at(place + k) if way else seq_at(place - k)
+            size = wouts[way].shape[0]
+            at = pl.multiple_of(origin * depth + starts[way], 16)
+            wfar[pl.ds(at, size), :] = lands[way][k].astype(BF16)
+        return carry
+
+    lax.fori_loop(0, seq, unpack, 0)
+
+    def send_part(i, carry):
+        copy_g(2 * i).wait()
+        copy_g(2 * i + 1).wait()
+
+        def put(cols, part):
+            part_send[i, :, cols] = part_send[i, :, cols] + part
+
+        spread(rows_of(g_recv, i), wfar, put)
+        copy_p(i).start()
+        return carry
+
+    lax.fori_loop(0, half, send_part, 0)
 
     def finish(i, carry):
-        copy_y(i).wait()
-        rows = pl.ds(pl.multiple_of(i * CH, CH), CH)
-        grad_ref[rows, :] = (send_a[i] + recv_y[i]).astype(BF16)
-        return carry
-
-    lax.fori_loop(0, each, finish, 0)
+        copy_g(2 * (half + i)).wait()
+        copy_g(2 * (half + i) + 1).wait()
+        copy_p(i).wait()
+        rows = pl.ds(pl.multiple_of(i * 2 * CH, 2 * CH), 2 * CH)
+
+        def put(cols, part):
+            grad_ref[rows, cols] = (
+                part_own[i, :, cols] + part + part_recv[i, :, cols]
+            ).astype(BF16)
+
+        spread(rows_of(g_recv, half + i), wfar, put)
+        return carry
+
+    lax.fori_loop(0, half, finish, 0)
+
+    def drain(k, carry):
+        for way in (0, 1):
+            ring(way, k).wait_send()
+        return carry
+
+    for way in (0, 1):
+        cross(way).wait_send()
+    lax.fori_loop(0, seq - 1, drain, 0)
 
 
 def solution(mesh):
@@ -290,7 +386,9 @@
         blocks, each = length // CH, length // CH // tp
         tile = 2 * CH
         scale = 4.0 * math.sqrt(length * seq * dk / dv)
-        piece = (each, CH, width)
+        depth = width // seq
+        upper = (depth // 2 + 15) // 16 * 16
+        sizes = (upper, depth - upper)
         hbm = pl.BlockSpec(memory_space=pl.ANY)
         vmem = pl.BlockSpec(memory_space=pltpu.VMEM)
         dma = pltpu.SemaphoreType.DMA
@@ -315,9 +413,15 @@
                 pltpu.VMEM((seq, dv + PAD, dk), F32),
                 pltpu.VMEM((2, dv, dk), F32),
             ]
-            + [pltpu.VMEM(piece, F32)] * 6
+            + [pltpu.VMEM((size, 3 * dk + dv), F32) for size in sizes]
+            + [pltpu.VMEM((seq, size, 3 * dk + dv), F32) for size in sizes]
+            + [pltpu.VMEM((width, 3 * dk + dv), BF16)]
+            + [pltpu.VMEM((2 * each, CH, 3 * dk + dv), kind) for kind in (BF16, F32, F32)]
+            + [pltpu.VMEM((each // 2, 2 * CH, width), F32)] * 3
             + [dma((4,)), dma((2,)), dma((seq,)), dma((seq,))]
-            + [dma((each,))] * 6,
+            + [dma((2 * each,))] * 2
+            + [dma((each // 2,))] * 2
+            + [dma((2,)), dma((2, seq)), dma((2, seq))],
             compiler_params=pltpu.CompilerParams(
                 collective_id=0, has_side_effects=True, vmem_limit_bytes=VMEM_LIMIT
             ),

time: 172 us -> 126 us (0.73)
  Pallas kernels: 165 us -> 120 us
    pallas_call x1, Pallas kernels: 165 us -> 120 us  [body(): pl.pallas_call(functools.partial(kernel, seq, tp, dk, dv, tile, scale), o...]
where the time goes in v2:
time: 126 us; the launch traced here: 125 us
  Pallas kernels  120 us (95%)
  local copies, waits for them, and re-layouts  4.46 us (4%)
    pallas_call x1, Pallas kernels, body(): pl.pallas_call(functools.partial(kernel, seq, tp, dk, dv, tile, scale), o...  120 us
    unnamed x4, local copies, waits for them, and re-layouts  4.46 us

profile of v2, /device:TPU:9, one launch (start us, length us, event | category | flops | bytes accessed | tf_op | source)
XLA Modules:
  0.0 125.0 jit_solution(5723087212982963555)
XLA Ops:
  0.6 119.9 %shard_map.86 = (bf16[512,2560]{1,0:T(8,128)(2,1)}, f32[2048,128]{1,0:T(8,128)}) custom-call(bf16[2048,2560]{1,0:T(8,128)(2,1)} %tok.1, bf16[2560,128]{1,0:T(8,128)(2,1)} %wq.1, bf16[2560,128]{1,0:T(8,128)(2,1)} %wk.1, bf16[2560,256]{1,0:T(8,128)(2,1)} %wv.1, bf16[2560,128]{1,0:T(8,128)(2,1)} %wg.1, f32[1,128]{1,0:T(1,128)} %bitcast.1, ...), custom_call_target="tpu_custom_call" | custom-call | tf_op jit(solution)/shard_map/pallas_call | solution.py:395
  120.5 0.0 copy-start
  120.6 3.5 %copy.11 = bf16[512,2560]{1,0:T(8,128)(2,1)} copy(bf16[512,2560]{1,0:T(8,128)(2,1)} %get-tuple-element.4) | data formatting | bytes 5242880
  124.0 0.0 copy-done
  124.0 1.0 copy.12
Async XLA Ops:
  120.5 3.5 %copy-start = (f32[2048,128]{1,0:T(8,128)S(1)}, f32[2048,128]{1,0:T(8,128)}, u32[]{:S(2)}) copy-start(f32[2048,128]{1,0:T(8,128)} %get-tuple-element.5) | copy-start | bytes 3145732

commit v3 on v2

--- a/solution.py
+++ b/solution.py
@@ -34,13 +34,14 @@
     tok, wq, wk, wv, wg, rate_ref, dout_ref,
     grad_ref, sig_ref,
     wcat, xbuf, proj, sq_all, w_all, s_all, m_all, cl_all, msg, got, edge,
-    wout0, wout1, land0, land1, wfar, g_own, g_send, g_recv, part_own, part_send, part_recv,
+    wout0, wout1, wout2, wout3, land0, land1, land2, land3, wfar, g_own, g_send, g_recv, part_own, part_send, part_recv,
     w_sem, x_sem, msg_send, msg_recv, gs_sem, gr_sem, ps_sem, pr_sem, first_sem, ring_s, ring_r,
 ):
     me, rank = lax.axis_index("seq"), lax.axis_index("tp")
     length, width = dout_ref.shape[0], wcat.shape[0]
     blocks, tiles = length // CH, length // tile
     each = blocks // tp
+    half = each // 2
     core = rank + 1 - 2 * lax.rem(rank, 2)
     far = lax.rem(rank + 2, 4)
     far_core = lax.rem(core + 2, 4)
@@ -53,8 +54,8 @@
         return 2 * p + (p // half_ring) * (2 * seq - 1 - 4 * p)
 
     onward = (seq_at(place + 1), seq_at(place - 1))
-    wouts, lands = (wout0, wout1), (land0, land1)
-    starts = (0, wout0.shape[0])
+    wouts, lands = (wout0, wout1, wout2, wout3), (land0, land1, land2, land3)
+    starts = [sum(w.shape[0] for w in wouts[:n]) for n in range(4)]
 
     def cross(way):
         return pltpu.make_async_remote_copy(
@@ -66,12 +67,12 @@
     def ring(way, k):
         return pltpu.make_async_remote_copy(
             src_ref=lands[way].at[k], dst_ref=lands[way].at[k + 1], send_sem=ring_s.at[way, k],
-            recv_sem=ring_r.at[way, k + 1], device_id={"seq": onward[way]},
+            recv_sem=ring_r.at[way, k + 1], device_id={"seq": onward[way % 2]},
             device_id_type=pl.DeviceIdType.MESH,
         )
 
-    def pump(k):
-        for way in (0, 1):
+    def pump(k, part):
+        for way in (2 * part, 2 * part + 1):
             if isinstance(k, int) and k == 0:
                 cross(way).wait_recv()
             else:
@@ -115,12 +116,12 @@
     msg[1, pl.ds(0, dv), :] = zero_state
     for load in loads:
         load.wait()
-    for way in (0, 1):
+    for way in range(4):
         size = wouts[way].shape[0]
         at = pl.multiple_of(me * depth + starts[way], 16)
         wouts[way][...] = wcat[pl.ds(at, size), :].astype(F32)
     pl.semaphore_wait(barrier, seq + 1)
-    for way in (0, 1):
+    for way in range(4):
         cross(way).start()
 
     def project(t, total):
@@ -129,6 +130,10 @@
         @pl.when(t + 1 < tiles)
         def _():
             x_copy(t + 1, 1 - slot).start()
+
+        @pl.when(t == tiles - 2)
+        def _():
+            pump(0, 0)
 
         x_copy(t, slot).wait()
         out = mm(xbuf[slot], wcat[...], NN)
@@ -182,9 +187,9 @@
         return carry
 
     lax.fori_loop(1, seq, start_exchange, 0)
-    pump(0)
+    pump(0, 1)
     lax.fori_loop(1, seq, wait_exchange, 0)
-    pump(1)
+    pump(1, 0)
 
     edge[...] = jnp.zeros_like(edge)
 
@@ -268,6 +273,13 @@
             recv_sem=pr_sem.at[i], device_id={"tp": core}, device_id_type=pl.DeviceIdType.MESH,
         )
 
+    steps = iter([(k, part) for k in range(1, seq - 1) for part in (0, 1)][1:])
+
+    def pump_next():
+        k = next(steps, None)
+        if k is not None:
+            pump(*k)
+
     def away(chunk, base):
         def run(i, carry):
             for (lo, hi), part in zip(bounds, grads(chunk * each + i)):
@@ -275,7 +287,10 @@
             copy_g(base + i).start()
             return carry
 
-        lax.fori_loop(0, each, run, 0)
+        lax.fori_loop(0, half, run, 0)
+        pump_next()
+        lax.fori_loop(half, each, run, 0)
+        pump_next()
 
     def home(chunk, base):
         def run(i, carry):
@@ -283,28 +298,18 @@
                 g_own[base + i, :, lo:hi] = part.astype(BF16)
             return carry
 
-        lax.fori_loop(0, each, run, 0)
-
-    steps = iter(range(2, seq - 1))
-
-    def pump_next():
-        k = next(steps, None)
-        if k is not None:
-            pump(k)
+        lax.fori_loop(0, half, run, 0)
+        pump_next()
+        lax.fori_loop(half, each, run, 0)
+        pump_next()
 
     def rows_of(buffer, i):
         return jnp.concatenate([buffer[2 * i], buffer[2 * i + 1]], axis=0).astype(BF16)
 
-    half = each // 2
-
     away(far_core, 0)
-    pump_next()
     away(far, each)
-    pump_next()
     home(core, 0)
-    pump_next()
     home(rank, each)
-    pump_next()
 
     def own_part(i, carry):
         def put_send(cols, part):
@@ -318,19 +323,23 @@
         return carry
 
     lax.fori_loop(0, half, own_part, 0)
-    done = next(steps, seq - 1)
+    done, part = next(steps, (seq - 1, 0))
+    if part == 1:
+        pump(done, 1)
+        done += 1
 
     def pump_rest(k, carry):
-        pump(k)
+        pump(k, 0)
+        pump(k, 1)
         return carry
 
     lax.fori_loop(done, seq - 1, pump_rest, 0)
-    for way in (0, 1):
+    for way in range(4):
         ring(way, seq - 2).wait_recv()
 
     def unpack(k, carry):
-        for way in (0, 1):
-            origin = seq_at(place + k) if way else seq_at(place - k)
+        for way in range(4):
+            origin = seq_at(place + k) if way % 2 else seq_at(place - k)
             size = wouts[way].shape[0]
             at = pl.multiple_of(origin * depth + starts[way], 16)
             wfar[pl.ds(at, size), :] = lands[way][k].astype(BF16)
@@ -368,11 +377,11 @@
     lax.fori_loop(0, half, finish, 0)
 
     def drain(k, carry):
-        for way in (0, 1):
+        for way in range(4):
             ring(way, k).wait_send()
         return carry
 
-    for way in (0, 1):
+    for way in range(4):
         cross(way).wait_send()
     lax.fori_loop(0, seq - 1, drain, 0)
 
@@ -387,8 +396,8 @@
         tile = 2 * CH
         scale = 4.0 * math.sqrt(length * seq * dk / dv)
         depth = width // seq
-        upper = (depth // 2 + 15) // 16 * 16
-        sizes = (upper, depth - upper)
+        units = depth // 16
+        sizes = [16 * ((units + 3 - n) // 4) for n in range(4)]
         hbm = pl.BlockSpec(memory_space=pl.ANY)
         vmem = pl.BlockSpec(memory_space=pltpu.VMEM)
         dma = pltpu.SemaphoreType.DMA
@@ -421,7 +430,7 @@
             + [dma((4,)), dma((2,)), dma((seq,)), dma((seq,))]
             + [dma((2 * each,))] * 2
             + [dma((each // 2,))] * 2
-            + [dma((2,)), dma((2, seq)), dma((2, seq))],
+            + [dma((4,)), dma((4, seq)), dma((4, seq))],
             compiler_params=pltpu.CompilerParams(
                 collective_id=0, has_side_effects=True, vmem_limit_bytes=VMEM_LIMIT
             ),

time: 126 us -> 121 us (0.960)
  Pallas kernels: 120 us -> 116 us
    pallas_call x1, Pallas kernels: 120 us -> 116 us  [body(): pl.pallas_call(functools.partial(kernel, seq, tp, dk, dv, tile, scale), o...]
where the time goes in v3:
time: 121 us
  Pallas kernels  116 us (96%)
  local copies, waits for them, and re-layouts  4.46 us (4%)
    pallas_call x1, Pallas kernels, body(): pl.pallas_call(functools.partial(kernel, seq, tp, dk, dv, tile, scale), o...  116 us
    unnamed x4, local copies, waits for them, and re-layouts  4.46 us

profile of v3, /device:TPU:9, one launch (start us, length us, event | category | flops | bytes accessed | tf_op | source)
XLA Modules:
  0.0 120.8 jit_solution(14152521826637850497)
XLA Ops:
  0.6 115.7 %shard_map.86 = (bf16[512,2560]{1,0:T(8,128)(2,1)}, f32[2048,128]{1,0:T(8,128)}) custom-call(bf16[2048,2560]{1,0:T(8,128)(2,1)} %tok.1, bf16[2560,128]{1,0:T(8,128)(2,1)} %wq.1, bf16[2560,128]{1,0:T(8,128)(2,1)} %wk.1, bf16[2560,256]{1,0:T(8,128)(2,1)} %wv.1, bf16[2560,128]{1,0:T(8,128)(2,1)} %wg.1, f32[1,128]{1,0:T(1,128)} %bitcast.1, ...), custom_call_target="tpu_custom_call" | custom-call | tf_op jit(solution)/shard_map/pallas_call | solution.py:404
  116.4 0.0 copy-start
  116.4 3.5 %copy.11 = bf16[512,2560]{1,0:T(8,128)(2,1)} copy(bf16[512,2560]{1,0:T(8,128)(2,1)} %get-tuple-element.4) | data formatting | bytes 5242880
  119.9 0.0 copy-done
  119.9 1.0 copy.12
Async XLA Ops:
  116.4 3.5 %copy-start = (f32[2048,128]{1,0:T(8,128)S(1)}, f32[2048,128]{1,0:T(8,128)}, u32[]{:S(2)}) copy-start(f32[2048,128]{1,0:T(8,128)} %get-tuple-element.5) | copy-start | bytes 3145732

commit v4 on v3

--- a/solution.py
+++ b/solution.py
@@ -334,9 +334,6 @@
         return carry
 
     lax.fori_loop(done, seq - 1, pump_rest, 0)
-    for way in range(4):
-        ring(way, seq - 2).wait_recv()
-
     def unpack(k, carry):
         for way in range(4):
             origin = seq_at(place + k) if way % 2 else seq_at(place - k)
@@ -345,7 +342,10 @@
             wfar[pl.ds(at, size), :] = lands[way][k].astype(BF16)
         return carry
 
-    lax.fori_loop(0, seq, unpack, 0)
+    lax.fori_loop(0, seq - 1, unpack, 0)
+    for way in range(4):
+        ring(way, seq - 2).wait_recv()
+    unpack(seq - 1, 0)
 
     def send_part(i, carry):
         copy_g(2 * i).wait()

time: 121 us -> 121 us (level)
  no operation moved by 1% of the time
where the time goes in v4:
time: 121 us; the launch traced here: 120 us
  Pallas kernels  115 us (95%)
  local copies, waits for them, and re-layouts  4.46 us (4%)
    pallas_call x1, Pallas kernels, body(): pl.pallas_call(functools.partial(kernel, seq, tp, dk, dv, tile, scale), o...  115 us
    unnamed x4, local copies, waits for them, and re-layouts  4.46 us

profile of v4, /device:TPU:9, one launch (start us, length us, event | category | flops | bytes accessed | tf_op | source)
XLA Modules:
  0.0 120.5 jit_solution(1448660042640231521)
XLA Ops:
  0.6 115.3 %shard_map.86 = (bf16[512,2560]{1,0:T(8,128)(2,1)}, f32[2048,128]{1,0:T(8,128)}) custom-call(bf16[2048,2560]{1,0:T(8,128)(2,1)} %tok.1, bf16[2560,128]{1,0:T(8,128)(2,1)} %wq.1, bf16[2560,128]{1,0:T(8,128)(2,1)} %wk.1, bf16[2560,256]{1,0:T(8,128)(2,1)} %wv.1, bf16[2560,128]{1,0:T(8,128)(2,1)} %wg.1, f32[1,128]{1,0:T(1,128)} %bitcast.1, ...), custom_call_target="tpu_custom_call" | custom-call | tf_op jit(solution)/shard_map/pallas_call | solution.py:404
  116.0 0.0 copy-start
  116.0 3.5 %copy.11 = bf16[512,2560]{1,0:T(8,128)(2,1)} copy(bf16[512,2560]{1,0:T(8,128)(2,1)} %get-tuple-element.4) | data formatting | bytes 5242880
  119.5 0.0 copy-done
  119.5 1.0 copy.12
Async XLA Ops:
  116.0 3.5 %copy-start = (f32[2048,128]{1,0:T(8,128)S(1)}, f32[2048,128]{1,0:T(8,128)}, u32[]{:S(2)}) copy-start(f32[2048,128]{1,0:T(8,128)} %get-tuple-element.5) | copy-start | bytes 3145732

commit v5 on v3

--- a/solution.py
+++ b/solution.py
@@ -189,7 +189,6 @@
     lax.fori_loop(1, seq, start_exchange, 0)
     pump(0, 1)
     lax.fori_loop(1, seq, wait_exchange, 0)
-    pump(1, 0)
 
     edge[...] = jnp.zeros_like(edge)
 
@@ -273,7 +272,7 @@
             recv_sem=pr_sem.at[i], device_id={"tp": core}, device_id_type=pl.DeviceIdType.MESH,
         )
 
-    steps = iter([(k, part) for k in range(1, seq - 1) for part in (0, 1)][1:])
+    steps = iter([(k, part) for k in range(1, seq - 1) for part in (0, 1)])
 
     def pump_next():
         k = next(steps, None)

time: 121 us -> 121 us (level)
  no operation moved by 1% of the time
where the time goes in v5:
time: 121 us
  Pallas kernels  116 us (96%)
  local copies, waits for them, and re-layouts  4.46 us (4%)
    pallas_call x1, Pallas kernels, body(): pl.pallas_call(functools.partial(kernel, seq, tp, dk, dv, tile, scale), o...  116 us
    unnamed x4, local copies, waits for them, and re-layouts  4.46 us

profile of v5, /device:TPU:9, one launch (start us, length us, event | category | flops | bytes accessed | tf_op | source)
XLA Modules:
  0.0 120.8 jit_solution(17843614640848164278)
XLA Ops:
  0.6 115.7 %shard_map.86 = (bf16[512,2560]{1,0:T(8,128)(2,1)}, f32[2048,128]{1,0:T(8,128)}) custom-call(bf16[2048,2560]{1,0:T(8,128)(2,1)} %tok.1, bf16[2560,128]{1,0:T(8,128)(2,1)} %wq.1, bf16[2560,128]{1,0:T(8,128)(2,1)} %wk.1, bf16[2560,256]{1,0:T(8,128)(2,1)} %wv.1, bf16[2560,128]{1,0:T(8,128)(2,1)} %wg.1, f32[1,128]{1,0:T(1,128)} %bitcast.1, ...), custom_call_target="tpu_custom_call" | custom-call | tf_op jit(solution)/shard_map/pallas_call | solution.py:403
  116.4 0.0 copy-start
  116.4 3.5 %copy.11 = bf16[512,2560]{1,0:T(8,128)(2,1)} copy(bf16[512,2560]{1,0:T(8,128)(2,1)} %get-tuple-element.4) | data formatting | bytes 5242880
  119.9 0.0 copy-done
  119.9 1.0 copy.12
Async XLA Ops:
  116.4 3.5 %copy-start = (f32[2048,128]{1,0:T(8,128)S(1)}, f32[2048,128]{1,0:T(8,128)}, u32[]{:S(2)}) copy-start(f32[2048,128]{1,0:T(8,128)} %get-tuple-element.5) | copy-start | bytes 3145732
